TPU v7x, 32 devices: a whole 2x2x4 slice. The times are simulated.
32 devices in a mesh: expert: 4 (over x, core), rows: 8 (over z, y).
Axes of the slice: x: 2, y: 2, z: 4, core: 2. Of those that a mesh axis runs over, the one named last changes fastest.
Arguments:
- step: int32 [], replicated, may hold values from 2 to 8
- gradient: bfloat16 [4, 4096, 14336], P('expert', 'rows'), may hold values from -8 to 8
- weight: bfloat16 [4, 4096, 14336], P('expert', 'rows'), may hold values from -0.119628906 to 0.119628906
- row_state: float32 [4, 4096], P('expert', 'rows'), may hold values from 0.3 to 3
- col_state: float32 [4, 14336], P('expert', 'rows'), may hold values from 0.3 to 3
- prev_msq: float32 [4, 8], P('expert', 'rows'), may hold values from 2 to 500
Outputs:
- new_weight: bfloat16 [4, 4096, 14336], P('expert', 'rows')
- new_row_state: float32 [4, 4096], P('expert', 'rows')
- new_col_state: float32 [4, 14336], P('expert', 'rows')
- new_msq: float32 [4, 8], P('expert', 'rows')
All inputs are finite; a program needn't handle non-finite values.
Results may differ from a plain program's by a relative error of at most 0.001.
Values sent between devices are 32-bit elements; how exact they have to be, the bound alone decides.
A program may use at most 128 MiB of HBM per device.

v0:
```python
import jax
import jax.numpy as jnp
from jax import lax
from jax.sharding import PartitionSpec as P


def shards(step, gradient, weight, row_state, col_state, prev_msq):
    local_experts = gradient.shape[0]
    local_rows = gradient.shape[1]
    columns = gradient.shape[2]
    row_devices = lax.axis_size("rows")
    expert_devices = lax.axis_size("expert")
    all_rows = local_rows * row_devices
    beta = 1.0 - step.astype(jnp.float32) ** (-0.8)
    grad = gradient.astype(jnp.float32)
    squares = grad * grad + 1e-30
    new_row = beta * row_state + (1.0 - beta) * jnp.mean(squares, axis=2)
    partial_cols = jnp.sum(squares, axis=1)
    clip_term = jnp.sum(prev_msq)
    row_sum = jnp.sum(new_row, axis=1)
    clip_total = lax.psum(clip_term, ("expert", "rows"))
    row_totals = lax.psum(row_sum, "rows")
    entries = prev_msq.shape[0] * prev_msq.shape[1] * expert_devices * row_devices
    clip = jnp.sqrt(clip_total / entries)
    row_mean = row_totals / all_rows
    old_full = lax.all_gather(col_state, "rows", axis=1, tiled=True)
    col_totals = lax.psum(partial_cols, "rows")
    full_cols = beta * old_full + (1.0 - beta) * col_totals / all_rows
    width = columns // row_devices
    new_col = lax.dynamic_slice_in_dim(full_cols, lax.axis_index("rows") * width, width, 1)
    scaled = new_row[:, :, None] * full_cols[:, None, :] / row_mean[:, None, None]
    update = grad / jnp.sqrt(scaled) / clip
    new_weight = (weight.astype(jnp.float32) - 0.01 * update).astype(jnp.bfloat16)
    new_msq = jnp.mean(update * update, axis=(1, 2)).reshape(local_experts, 1)
    return (new_weight, new_row, new_col, new_msq)


def solution(mesh):
    placed = (
        P(),
        P("expert", "rows", None),
        P("expert", "rows", None),
        P("expert", "rows"),
        P("expert", "rows"),
        P("expert", "rows"),
    )
    return jax.shard_map(
        shards,
        mesh=mesh,
        in_specs=placed,
        out_specs=(
            P("expert", "rows", None),
            P("expert", "rows"),
            P("expert", "rows"),
            P("expert", "rows"),
        ),
        check_vma=False,
    )
```

profile of v0, /device:TPU:14, one launch (start us, length us, event | category | flops | bytes accessed | tf_op | source)
XLA Modules:
  0.0 155.5 jit_solution(15498681350571910622)
XLA Ops:
  0.6 0.0 copy-start.2
  0.6 0.0 copy-start.1
  1.4 20.0 %fusion.1 = (f32[14336]{0:T(1024)S(1)}, f32[512]{0:T(512)S(1)}) fusion(bf16[1,512,14336]{2,1,0:T(8,128)(2,1)} %param.7), kind=kLoop, calls=%fused_computation.3 | loop fusion | flops 36685312 | bytes 14739456 | tf_op jit(solution)/shard_map/reduce_sum | solution.py:18
  21.4 0.0 copy-done.2
  21.4 0.6 fusion.4
  22.0 0.0 copy-start
  22.0 31.1 %all-reduce = (f32[1]{0:T(128)}, f32[1,14336]{1,0:T(1,128)S(1)}) all-reduce(f32[1]{0:T(128)} %bitcast.4, f32[1,14336]{1,0:T(1,128)S(1)} %bitcast.9), channel_id=1, replica_groups=mesh['expert'=4,'rows'=8] {'rows'}, use_global_device_ids=true, to_apply=%region_4.0 | all-reduce | flops 14337 | bytes 114696 | tf_op jit(solution)/shard_map/psum | solution.py:22
  53.1 0.0 copy-done.1
  53.1 30.4 %all_gather.3 = f32[1,14336]{1,0:T(1,128)S(1)} all-gather(f32[1,1792]{1,0:T(1,128)S(1)} %copy-done.1), channel_id=1, replica_groups=mesh['expert'=4,'rows'=8] {'rows'}, dimensions={1}, use_global_device_ids=true | all-gather | bytes 64512 | tf_op jit(solution)/shard_map/all_gather | solution.py:26
  83.5 0.1 multiply_add_fusion
  84.2 46.5 %psum.23 = f32[]{:T(128)} all-reduce(f32[]{:T(128)} %bitcast.6), channel_id=1, replica_groups=mesh['expert'=4,'rows'=8] {'expert','rows'}, use_global_device_ids=true, to_apply=%region_5.0 | all-reduce | flops 1 | bytes 8 | tf_op jit(solution)/shard_map/psum | solution.py:21
  131.4 21.7 %multiply_reduce_fusion = (f32[]{:T(128)}, bf16[1,512,14336]{2,1,0:T(8,128)(2,1)}) fusion(f32[]{:T(128)S(6)} %sqrt.7, f32[]{:T(128)} %bitcast.5, f32[14336]{0:T(1024)S(1)} %bitcast.8, f32[512]{0:T(512)S(1)} %bitcast.10, bf16[1,512,14336]{2,1,0:T(8,128)(2,1)} %param.7, bf16[1,512,14336]{2,1,0:T(8,128)(2,1)} %param.8), kind=kLoop, calls=%fused_computation.6 | loop fusion | flops 80740352 | bytes 44099596 | tf_op jit(solution)/shard_map/reduce_sum | solution.py:34
  153.1 0.0 copy-done
  153.8 0.6 constant_dynamic-slice_fusion
  (1 shorter events, 0.0 us)
Async XLA Ops:
  0.6 20.8 %copy-start.2 = (f32[1,512]{1,0:T(1,128)S(1)}, f32[1,512]{1,0:T(1,128)}, u32[]{:S(2)}) copy-start(f32[1,512]{1,0:T(1,128)} %param.9) | copy-start | bytes 6148
  0.6 52.5 %copy-start.1 = (f32[1,1792]{1,0:T(1,128)S(1)}, f32[1,1792]{1,0:T(1,128)}, u32[]{:S(2)}) copy-start(f32[1,1792]{1,0:T(1,128)} %param.10) | copy-start | bytes 21508
  22.0 131.1 %copy-start = (f32[1,512]{1,0:T(1,128)}, f32[1,512]{1,0:T(1,128)S(1)}, u32[]{:S(2)}) copy-start(f32[1,512]{1,0:T(1,128)S(1)} %get-tuple-element.9) | copy-start | bytes 6148
where the time goes:
time: 156 us; the launch traced here: 155 us
  blocking collectives  108 us (69%)
  other arithmetic  42.4 us (27%)
  between operations  4.52 us (3%)
    psum x1, blocking collectives, shards(): clip_total = lax.psum(clip_term, ('expert', 'rows'))  46.5 us
    psum x1, blocking collectives, shards(): row_totals = lax.psum(row_sum, 'rows')  31.1 us
    all_gather x1, blocking collectives, shards(): old_full = lax.all_gather(col_state, 'rows', axis=1, tiled=True)  30.4 us
    reduce_sum x1, other arithmetic, shards(): new_msq = jnp.mean(update * update, axis=(1, 2)).reshape(local_experts, 1)  21.7 us
    reduce_sum x1, other arithmetic, shards(): partial_cols = jnp.sum(squares, axis=1)  20 us

commit v1 on v0

--- a/solution.py
+++ b/solution.py
@@ -23,7 +23,8 @@
     entries = prev_msq.shape[0] * prev_msq.shape[1] * expert_devices * row_devices
     clip = jnp.sqrt(clip_total / entries)
     row_mean = row_totals / all_rows
-    old_full = lax.all_gather(col_state, "rows", axis=1, tiled=True)
+    parts = lax.all_gather(col_state, "rows", axis=0, tiled=False)
+    old_full = jnp.concatenate(parts, axis=1)
     col_totals = lax.psum(partial_cols, "rows")
     full_cols = beta * old_full + (1.0 - beta) * col_totals / all_rows
     width = columns // row_devices

time: 156 us -> 156 us (level)
  no operation moved by 1% of the time
where the time goes in v1:
time: 156 us
  blocking collectives  108 us (69%)
  other arithmetic  42.4 us (27%)
  between operations  4.53 us (3%)
    psum x1, blocking collectives, shards(): clip_total = lax.psum(clip_term, ('expert', 'rows'))  46.5 us
    psum x1, blocking collectives, shards(): row_totals = lax.psum(row_sum, 'rows')  31.1 us
    all_gather x1, blocking collectives, shards(): parts = lax.all_gather(col_state, 'rows', axis=0, tiled=False)  30.4 us
    reduce_sum x1, other arithmetic, shards(): new_msq = jnp.mean(update * update, axis=(1, 2)).reshape(local_experts, 1)  21.7 us
    reduce_sum x1, other arithmetic, shards(): partial_cols = jnp.sum(squares, axis=1)  20 us

profile of v1, /device:TPU:14, one launch (start us, length us, event | category | flops | bytes accessed | tf_op | source)
XLA Modules:
  0.0 155.5 jit_solution(936862337444378082)
XLA Ops:
  0.6 0.0 copy-start.2
  0.6 0.0 copy-start.1
  1.4 20.0 %fusion.1 = (f32[14336]{0:T(1024)S(1)}, f32[512]{0:T(512)S(1)}) fusion(bf16[1,512,14336]{2,1,0:T(8,128)(2,1)} %param.7), kind=kLoop, calls=%fused_computation.3 | loop fusion | flops 36685312 | bytes 14739456 | tf_op jit(solution)/shard_map/reduce_sum | solution.py:18
  21.4 0.0 copy-done.2
  21.4 0.6 fusion.4
  22.0 0.0 copy-start
  22.0 31.1 %all-reduce = (f32[1]{0:T(128)}, f32[1,14336]{1,0:T(1,128)S(1)}) all-reduce(f32[1]{0:T(128)} %bitcast.6, f32[1,14336]{1,0:T(1,128)S(1)} %bitcast.13), channel_id=1, replica_groups=mesh['expert'=4,'rows'=8] {'rows'}, use_global_device_ids=true, to_apply=%region_4.0 | all-reduce | flops 14337 | bytes 114696 | tf_op jit(solution)/shard_map/psum | solution.py:22
  53.1 0.0 copy-done.1
  53.1 30.4 %all-gather.1 = f32[8,1,1792]{2,1,0:T(1,128)S(1)} all-gather(f32[1,1,1792]{2,1,0:T(1,128)S(1)} %bitcast.18), channel_id=2, replica_groups=mesh['expert'=4,'rows'=8] {'rows'}, dimensions={0}, use_global_device_ids=true | all-gather | bytes 64512 | tf_op jit(solution)/shard_map/all_gather | solution.py:26
  83.5 0.1 multiply_add_fusion
  84.3 46.5 %psum.23 = f32[]{:T(128)} all-reduce(f32[]{:T(128)} %bitcast.8), channel_id=1, replica_groups=mesh['expert'=4,'rows'=8] {'expert','rows'}, use_global_device_ids=true, to_apply=%region_5.0 | all-reduce | flops 1 | bytes 8 | tf_op jit(solution)/shard_map/psum | solution.py:21
  131.4 21.7 %multiply_reduce_fusion = (f32[]{:T(128)}, bf16[1,512,14336]{2,1,0:T(8,128)(2,1)}) fusion(f32[]{:T(128)S(6)} %sqrt.7, f32[]{:T(128)} %bitcast.7, f32[14336]{0:T(1024)S(1)} %bitcast.12, f32[512]{0:T(512)S(1)} %bitcast.16, bf16[1,512,14336]{2,1,0:T(8,128)(2,1)} %param.7, bf16[1,512,14336]{2,1,0:T(8,128)(2,1)} %param.8), kind=kLoop, calls=%fused_computation.6 | loop fusion | flops 80740352 | bytes 44099596 | tf_op jit(solution)/shard_map/reduce_sum | solution.py:35
  153.1 0.0 copy-done
  153.8 0.6 constant_dynamic-slice_fusion
  (2 shorter events, 0.0 us)
Async XLA Ops:
  0.6 20.8 %copy-start.2 = (f32[1,512]{1,0:T(1,128)S(1)}, f32[1,512]{1,0:T(1,128)}, u32[]{:S(2)}) copy-start(f32[1,512]{1,0:T(1,128)} %param.9) | copy-start | bytes 6148
  0.6 52.5 %copy-start.1 = (f32[1,1792]{1,0:T(1,128)S(1)}, f32[1,1792]{1,0:T(1,128)}, u32[]{:S(2)}) copy-start(f32[1,1792]{1,0:T(1,128)} %param.10) | copy-start | bytes 21508
  22.0 131.1 %copy-start = (f32[1,512]{1,0:T(1,128)}, f32[1,512]{1,0:T(1,128)S(1)}, u32[]{:S(2)}) copy-start(f32[1,512]{1,0:T(1,128)S(1)} %get-tuple-element.9) | copy-start | bytes 6148

commit v2 on v0

--- a/solution.py
+++ b/solution.py
@@ -19,7 +19,10 @@
     clip_term = jnp.sum(prev_msq)
     row_sum = jnp.sum(new_row, axis=1)
     clip_total = lax.psum(clip_term, ("expert", "rows"))
-    row_totals = lax.psum(row_sum, "rows")
+    size, row_totals = (lax.axis_size("rows"), row_sum)
+    for stride in [1 << k for k in range(size.bit_length() - 1)]:
+        swap = [(i, i ^ stride) for i in range(size)]
+        row_totals = row_totals + lax.ppermute(row_totals, "rows", swap)
     entries = prev_msq.shape[0] * prev_msq.shape[1] * expert_devices * row_devices
     clip = jnp.sqrt(clip_total / entries)
     row_mean = row_totals / all_rows

time: 156 us -> 167 us (1.071)
  waiting for transfers between devices: 0 us -> 5.25 us
  starting transfers between devices: 0 us -> 3.33 us
  between operations: 4.52 us -> 6.66 us
    ppermute x0 -> x3, waiting for transfers between devices: none -> 5.25 us  [shards(): row_totals = row_totals + lax.ppermute(row_totals, 'rows', swap)]
    ppermute x0 -> x3, starting transfers between devices: none -> 3.33 us  [shards(): row_totals = row_totals + lax.ppermute(row_totals, 'rows', swap)]
  transfers between devices with their start and end apart: 0 -> 3, of which waited for: 0 -> 2; matrix products, arithmetic and copies ran while one was open for 0% -> 0% of each run, Pallas kernels for 0% -> 0%
where the time goes in v2:
time: 167 us; the launch traced here: 166 us
  blocking collectives  108 us (65%)
  other arithmetic  42.5 us (25%)
  between operations  6.66 us (4%)
  waiting for transfers between devices  5.25 us (3%)
  starting transfers between devices  3.33 us (2%)
    psum x1, blocking collectives, shards(): clip_total = lax.psum(clip_term, ('expert', 'rows'))  46.4 us
    all_gather x1, blocking collectives, shards(): old_full = lax.all_gather(col_state, 'rows', axis=1, tiled=True)  30.8 us
    psum x1, blocking collectives, shards(): col_totals = lax.psum(partial_cols, 'rows')  30.8 us
    reduce_sum x1, other arithmetic, shards(): new_msq = jnp.mean(update * update, axis=(1, 2)).reshape(local_experts, 1)  21.8 us
    reduce_sum x1, other arithmetic, shards(): partial_cols = jnp.sum(squares, axis=1)  20 us
    ppermute x3, waiting for transfers between devices, shards(): row_totals = row_totals + lax.ppermute(row_totals, 'rows', swap)  5.25 us
  transfers between devices with their start and end apart: 3, of which 2 were waited for; matrix products, arithmetic and copies ran while one was open for 0% of the time, Pallas kernels for 0%

profile of v2, /device:TPU:14, one launch (start us, length us, event | category | flops | bytes accessed | tf_op | source)
XLA Modules:
  0.0 166.3 jit_solution(4603503199658933721)
XLA Ops:
  0.6 0.0 copy-start.2
  0.6 0.0 copy-start.1
  1.4 20.0 %fusion.1 = (f32[14336]{0:T(1024)S(1)}, f32[512]{0:T(512)S(1)}) fusion(bf16[1,512,14336]{2,1,0:T(8,128)(2,1)} %param.7), kind=kLoop, calls=%fused_computation.3 | loop fusion | flops 36685312 | bytes 14739456 | tf_op jit(solution)/shard_map/reduce_sum | solution.py:18
  21.4 0.0 copy-done.2
  21.4 0.6 fusion.4
  22.0 0.0 copy-start
  22.0 0.5 collective-permute-start
  22.5 30.8 %psum.14 = f32[1,14336]{1,0:T(1,128)S(1)} all-reduce(f32[1,14336]{1,0:T(1,128)S(1)} %bitcast.9), channel_id=1, replica_groups=mesh['expert'=4,'rows'=8] {'rows'}, use_global_device_ids=true, to_apply=%region_2.0 | all-reduce | flops 14336 | bytes 114688 | tf_op jit(solution)/shard_map/psum | solution.py:30
  53.3 0.0 copy-done.1
  53.3 30.8 %all_gather.3 = f32[1,14336]{1,0:T(1,128)S(1)} all-gather(f32[1,1792]{1,0:T(1,128)S(1)} %copy-done.1), channel_id=1, replica_groups=mesh['expert'=4,'rows'=8] {'rows'}, dimensions={1}, use_global_device_ids=true | all-gather | bytes 64512 | tf_op jit(solution)/shard_map/all_gather | solution.py:29
  84.1 46.4 %psum.15 = f32[]{:T(128)} all-reduce(f32[]{:T(128)} %bitcast.6), channel_id=1, replica_groups=mesh['expert'=4,'rows'=8] {'expert','rows'}, use_global_device_ids=true, to_apply=%region_4.0 | all-reduce | flops 1 | bytes 8 | tf_op jit(solution)/shard_map/psum | solution.py:21
  131.2 0.1 multiply_add_fusion
  131.3 0.6 constant_dynamic-slice_fusion
  131.9 0.0 collective-permute-done
  133.2 1.4 collective-permute-start.1
  134.6 2.2 %collective-permute-done.1 = f32[1]{0:T(128)} collective-permute-done((f32[1]{0:T(128)}, f32[1]{0:T(128)}, u32[]{:S(2)}, u32[]{:S(2)}) %collective-permute-start.1) | collective-permute-done | bytes 36 | tf_op jit(solution)/shard_map/ppermute | solution.py:25
  137.5 1.5 collective-permute-start.2
  139.0 3.0 %collective-permute-done.2 = f32[1]{0:T(128)} collective-permute-done((f32[1]{0:T(128)}, f32[1]{0:T(128)}, u32[]{:S(2)}, u32[]{:S(2)}) %collective-permute-start.2) | collective-permute-done | bytes 36 | tf_op jit(solution)/shard_map/ppermute | solution.py:25
  142.7 21.8 %multiply_reduce_fusion = (f32[]{:T(128)}, bf16[1,512,14336]{2,1,0:T(8,128)(2,1)}) fusion(f32[]{:T(128)S(6)} %sqrt.7, f32[]{:T(128)} %bitcast.5, f32[14336]{0:T(1024)S(1)} %bitcast.8, f32[512]{0:T(512)S(1)} %bitcast.10, bf16[1,512,14336]{2,1,0:T(8,128)(2,1)} %param.7, bf16[1,512,14336]{2,1,0:T(8,128)(2,1)} %param.8), kind=kLoop, calls=%fused_computation.6 | loop fusion | flops 80740352 | bytes 44099596 | tf_op jit(solution)/shard_map/reduce_sum | solution.py:37
  164.5 0.0 copy-done
  (1 shorter events, 0.0 us)
Async XLA Ops:
  0.6 20.8 %copy-start.2 = (f32[1,512]{1,0:T(1,128)S(1)}, f32[1,512]{1,0:T(1,128)}, u32[]{:S(2)}) copy-start(f32[1,512]{1,0:T(1,128)} %param.9) | copy-start | bytes 6148
  0.6 52.6 %copy-start.1 = (f32[1,1792]{1,0:T(1,128)S(1)}, f32[1,1792]{1,0:T(1,128)}, u32[]{:S(2)}) copy-start(f32[1,1792]{1,0:T(1,128)} %param.10) | copy-start | bytes 21508
  22.0 142.4 %copy-start = (f32[1,512]{1,0:T(1,128)}, f32[1,512]{1,0:T(1,128)S(1)}, u32[]{:S(2)}) copy-start(f32[1,512]{1,0:T(1,128)S(1)} %get-tuple-element.7) | copy-start | bytes 6148
  22.0 109.9 %collective-permute-start = (f32[1]{0:T(128)}, f32[1]{0:T(128)}, u32[]{:S(2)}, u32[]{:S(2)}) collective-permute-start(f32[1]{0:T(128)} %bitcast.4), channel_id=1, source_target_pairs={{0,1},{1,0},{2,3},{3,2},{4,5},{5,4},{6,7},{7,6},{8,9},{9,8},{10,11... | collective-permute-start | bytes 20 | tf_op jit(solution)/shard_map/ppermute | solution.py:25
  133.2 3.6 %collective-permute-start.1 = (f32[1]{0:T(128)}, f32[1]{0:T(128)}, u32[]{:S(2)}, u32[]{:S(2)}) collective-permute-start(f32[1]{0:T(128)} %add.35), channel_id=1, source_target_pairs={{0,2},{1,3},{2,0},{3,1},{4,6},{5,7},{6,4},{7,5},{8,10},{9,11},{10,... | collective-permute-start | bytes 20 | tf_op jit(solution)/shard_map/ppermute | solution.py:25
  137.5 4.5 %collective-permute-start.2 = (f32[1]{0:T(128)}, f32[1]{0:T(128)}, u32[]{:S(2)}, u32[]{:S(2)}) collective-permute-start(f32[1]{0:T(128)} %add.36), channel_id=1, source_target_pairs={{0,4},{1,5},{2,6},{3,7},{4,0},{5,1},{6,2},{7,3},{8,12},{9,13},{10,... | collective-permute-start | bytes 20 | tf_op jit(solution)/shard_map/ppermute | solution.py:25
